TPU v7x, 32 devices: a whole 2x2x4 slice. The times are simulated.
32 devices in a mesh: groups: 2 (over y), gx: 4 (over z), gy: 2 (over x), gz: 2 (over core).
Axes of the slice: x: 2, y: 2, z: 4, core: 2. Of those that a mesh axis runs over, the one named last changes fastest.
Arguments:
- latents: bfloat16 [8, 2, 2, 128, 128], P(('groups', 'gx'), 'gy', 'gz'), parts along dimension 0, may hold values from -6 to 6
- offsets: bfloat16 [8, 2, 2, 3, 128], P(('groups', 'gx'), 'gy', 'gz'), parts along dimension 0, may hold values from 0 to 1
- neighbours: int32 [8, 2, 2, 384], P(('groups', 'gx'), 'gy', 'gz'), parts along dimension 0, may hold values from 0 to 2047, as said below
- counts: int32 [8, 2, 2], P(('groups', 'gx'), 'gy', 'gz'), parts along dimension 0, may hold values from 1 to 384, as said below
- w_recv: bfloat16 [1, 128, 128], replicated, may hold values from -0.5 to 0.5
- w_send: bfloat16 [1, 128, 128], replicated, may hold values from -0.5 to 0.5
- w_rel: bfloat16 [1, 4, 128], replicated, may hold values from -3 to 3
- b_first: float32 [1, 128], replicated, may hold values from -5 to 5
- w_edge: bfloat16 [1, 128, 128], replicated, may hold values from -0.5 to 0.5
- b_edge: float32 [1, 128], replicated, may hold values from -5 to 5
- w_self: bfloat16 [1, 128, 128], replicated, may hold values from -0.5 to 0.5
- w_agg: bfloat16 [1, 128, 128], replicated, may hold values from -0.5 to 0.5
- w_out: bfloat16 [1, 128, 128], replicated, may hold values from -0.5 to 0.5
- norm_gain: float32 [1, 128], replicated, may hold values from 0.1 to 1.9
Outputs:
- processed: bfloat16 [8, 2, 2, 128, 128], P(('groups', 'gx'), 'gy', 'gz'), parts along dimension 0
There are 2 independent parts, one for each index of `groups`. A program takes and returns all parts, laid end to end along the dimension named above; an argument that names none is the same for every part. Nothing has to cross between parts.
Inputs may be any that keep to these rules, and one draw needn't show every extreme that they name: `neighbours`: each sender is a particle of the same cell or of a cell whose three coordinates differ from the receiver cell's by at most one. Only the first counts[cell] senders of a cell are live, the rest is padding. In the cells whose first coordinate is below 1 all 384 senders are live.
All inputs are finite; a program needn't handle non-finite values.
Results may differ from a plain program's by a relative error of at most 0.0055.
Values may be sent and summed in bfloat16 or wider, within the bound.
A program may use at most 64 MiB of HBM per device.

v0:
```python
import functools

import jax
import jax.numpy as jnp
from jax import lax
from jax.experimental import pallas as pl
from jax.experimental.pallas import tpu as pltpu
from jax.sharding import PartitionSpec as P

MESH = pl.DeviceIdType.MESH
PACK = 16
GROUP = 32
PAIRS = 1
INPUTS = 14
LOAD_ORDER = (1, 2, 3, 0) + tuple(range(4, 14))


def split(value, size):
    if size & (size - 1) == 0:
        return value >> (size.bit_length() - 1), value & (size - 1)
    return lax.div(value, size), lax.rem(value, size)


def wide(axis):
    return lax.axis_size(axis) > 2


def slots_of(axis):
    return min(lax.axis_size(axis), 3)


def moves(axis):
    size, here = lax.axis_size(axis), lax.axis_index(axis)
    if size == 1:
        return []
    if size == 2:
        return [(1 - here, None)]
    return [(here - 1, here > 0), (here + 1, here < size - 1)]


def slot_on(axis, source, target):
    return source - target + 1 if wide(axis) else source


def both(a, b):
    if a is None:
        return b
    return a if b is None else jnp.logical_and(a, b)


def guarded(condition, action):
    if condition is None:
        action()
    else:
        pl.when(condition)(action)


def kernel(*refs):
    hbm, out_ref, held, scratch = refs[:INPUTS], refs[INPUTS], refs[INPUTS + 1 : 2 * INPUTS + 1], refs[2 * INPUTS + 1 :]
    load_sem, table, recv_half, send_half, scaled, pooled, pair_edge, masked, chosen = scratch[:9]
    send_sem, recv_sem, relay_sem = scratch[9:]
    (
        counts_ref, latents_ref, offsets_ref, neighbours_ref, w_recv, w_send, w_rel, b_first,
        w_edge, b_edge, w_self, w_agg, w_out, norm_gain,
    ) = held
    loads = [
        pltpu.make_async_copy(src, dst, load_sem.at[n]) for n, (src, dst) in enumerate(zip(hbm, held))
    ]
    for n in LOAD_ORDER:
        loads[n].start()
    f32, bf16 = jnp.float32, jnp.bfloat16
    slots, width = latents_ref.shape[3], latents_ref.shape[4]
    senders = neighbours_ref.shape[3]
    blocks = senders // slots
    here = [lax.axis_index(axis) for axis in ("gx", "gy", "gz")]
    sizes = [lax.axis_size(axis) for axis in ("gx", "gy", "gz")]
    spans = [slots_of(axis) for axis in ("gx", "gy", "gz")]

    def slot(coords):
        return (coords[0] * spans[1] + coords[1]) * spans[2] + coords[2]

    own_coords = [slot_on(a, c, c) for a, c in zip(("gx", "gy", "gz"), here)]
    own = slot(own_coords)

    stay_x, stay_y = (here[0], None), (here[1], None)
    routes = []
    for x, when_x in [stay_x] + moves("gx"):
        for y, when_y in [stay_y] + moves("gy"):
            if x is here[0] and y is here[1]:
                continue
            routes.append((x, y, both(when_x, when_y)))
    routes.sort(key=lambda r: (r[0] is not here[0]) + (r[1] is not here[1]))
    has_mate = sizes[2] > 1
    mate = {"gz": 1 - here[2]}

    barrier = pltpu.get_barrier_semaphore()

    def hello(target):
        pl.semaphore_signal(barrier, inc=1, device_id=target, device_id_type=MESH)

    if has_mate:
        hello(mate)
    for x, y, when in routes:
        guarded(when, functools.partial(hello, {"gx": x, "gy": y}))
    for n in (1, 2):
        loads[n].wait()
    latent = latents_ref[0, 0, 0]
    place = offsets_ref[0, 0, 0].astype(f32)
    rows = lax.broadcasted_iota(jnp.int32, (PACK, slots), 0)
    extra = jnp.zeros((PACK, slots), f32)
    for c in range(3):
        extra = jnp.where(rows == c, place[c : c + 1, :], extra)
        extra = jnp.where(rows == 3 + c, here[c].astype(f32), extra)
    table[own, :slots, :] = latent
    table[own, slots:, :] = extra.astype(bf16)

    peers = jnp.int32(1 if has_mate else 0)
    for x, y, when in routes:
        peers = peers + (1 if when is None else when.astype(jnp.int32))
    pl.semaphore_wait(barrier, peers)

    sends, relays = [], []
    for n, (x, y, when) in enumerate(routes):
        there = slot(
            [slot_on("gx", here[0], x), slot_on("gy", here[1], y), slot_on("gz", here[2], here[2])]
        )
        mine = slot(
            [slot_on("gx", x, here[0]), slot_on("gy", y, here[1]), slot_on("gz", here[2], here[2])]
        )
        copy = pltpu.make_async_remote_copy(
            src_ref=table.at[own],
            dst_ref=table.at[there],
            send_sem=send_sem.at[n],
            recv_sem=recv_sem.at[there],
            device_id={"gx": x, "gy": y},
            device_id_type=MESH,
        )
        arrival = pltpu.make_async_remote_copy(
            src_ref=table.at[own],
            dst_ref=table.at[mine],
            send_sem=send_sem.at[n],
            recv_sem=recv_sem.at[mine],
            device_id={"gx": x, "gy": y},
            device_id_type=MESH,
        )
        relay = pltpu.make_async_remote_copy(
            src_ref=table.at[mine],
            dst_ref=table.at[mine],
            send_sem=relay_sem.at[n],
            recv_sem=recv_sem.at[mine],
            device_id=mate,
            device_id_type=MESH,
        )
        mate_slot = slot(
            [slot_on("gx", x, here[0]), slot_on("gy", y, here[1]), 1 - here[2]]
        )
        mate_arrival = pltpu.make_async_remote_copy(
            src_ref=table.at[own],
            dst_ref=table.at[mate_slot],
            send_sem=relay_sem.at[n],
            recv_sem=recv_sem.at[mate_slot],
            device_id=mate,
            device_id_type=MESH,
        )
        sends.append((when, copy, arrival, mine))
        relays.append((relay, mate_arrival, mate_slot))
    last = len(routes)
    if has_mate:
        mate_own = slot([own_coords[0], own_coords[1], 1 - here[2]])
        mate_copy = pltpu.make_async_remote_copy(
            src_ref=table.at[own], dst_ref=table.at[own], send_sem=send_sem.at[last],
            recv_sem=recv_sem.at[own], device_id=mate, device_id_type=MESH,
        )
        mate_in = pltpu.make_async_remote_copy(
            src_ref=table.at[own], dst_ref=table.at[mate_own], send_sem=send_sem.at[last],
            recv_sem=recv_sem.at[mate_own], device_id=mate, device_id_type=MESH,
        )
    for when, copy, _, _ in sends:
        guarded(when, copy.start)
    if has_mate:
        mate_copy.start()

    def clear(which):
        table[which] = jnp.zeros(table.shape[1:], bf16)

    for (when, _, _, mine), (_, _, mate_slot) in zip(sends, relays):
        if when is not None:
            pl.when(jnp.logical_not(when))(functools.partial(clear, mine))
            if has_mate:
                pl.when(jnp.logical_not(when))(functools.partial(clear, mate_slot))

    loads[0].wait()
    for n in range(3, INPUTS):
        loads[n].wait()
    cell, at = split(neighbours_ref[0, 0], slots)
    cell, z = split(cell, sizes[2])
    x, y = split(cell, sizes[1])
    found = [
        v - h + 1 if wide(a) else v for a, v, h in zip(("gx", "gy", "gz"), (x, y, z), here)
    ]
    row_ids = (slot(found) * slots + at).astype(f32)
    ids = jnp.concatenate(
        [
            jnp.broadcast_to(row_ids[:, b * slots : (b + 1) * slots], (slots, slots)).T
            for b in range(blocks)
        ],
        axis=0,
    ).astype(jnp.int32)
    lanes = lax.broadcasted_iota(jnp.int32, (senders, slots), 1)
    count = table.shape[0]
    span_z = spans[2]
    for k in range(count):
        chosen[k // span_z, :, (k % span_z) * slots : (k % span_z + 1) * slots] = jnp.where(
            ids - k * slots == lanes, 1.0, 0.0
        ).astype(bf16)

    rel = w_rel[0].astype(f32)
    place_cols = jnp.transpose(jnp.broadcast_to(place[:1], (slots, slots)))
    recv = jnp.dot(latent, w_recv[0], preferred_element_type=f32) + b_first[...]
    for c in range(3):
        if c:
            place_cols = jnp.transpose(jnp.broadcast_to(place[c : c + 1], (slots, slots)))
        recv = recv - place_cols * rel[c : c + 1]
    recv_half[...] = 0.5 * recv

    def gather(line, carry):
        picks, cells = chosen[line], table.at[pl.ds(line * span_z, span_z)]
        found = jnp.dot(
            picks, cells[:, :slots, :].reshape(span_z * slots, width), preferred_element_type=f32
        )
        marks = cells[:, slots:, :]
        marks = jnp.concatenate([marks[k] for k in range(span_z)], axis=1)
        feats = lax.dot_general(picks, marks, (((1,), (1,)), ((), ())), preferred_element_type=f32)
        return (found, feats) if carry is None else (carry[0] + found, carry[1] + feats)

    if has_mate:
        mate_in.wait_recv()
    carry = gather(slot([own_coords[0], own_coords[1], 0]) // span_z, None)
    for (when, _, arrival, _), (relay, _, _) in zip(sends, relays):

        def pass_on(arrival=arrival, relay=relay):
            arrival.wait_recv()
            if has_mate:
                relay.start()

        guarded(when, pass_on)
    for (when, _, _, mine), (_, mate_arrival, _) in zip(sends, relays):
        if has_mate:
            guarded(when, mate_arrival.wait_recv)
        carry = gather(mine // span_z, carry)
    gathered, feats = carry[0].astype(bf16), carry[1]
    send = jnp.dot(gathered, w_send[0], preferred_element_type=f32)
    square = jnp.zeros((senders, slots), f32)
    for c in range(3):
        where = feats[:, c : c + 1] + (feats[:, 3 + c : 4 + c] - here[c].astype(f32))
        where = jnp.broadcast_to(where, (senders, slots))
        send = send + where * rel[c : c + 1]
        apart = where - place[c : c + 1]
        square = square + apart * apart
    send_half[...] = (0.5 * send).astype(bf16)
    square = 0.25 * square
    scaled[...] = jnp.transpose(square)

    rel_half = (0.5 * rel[3:4]).astype(bf16)
    edge_half = 0.5 * w_edge[0].astype(f32)
    nil = jnp.zeros_like(edge_half)
    pair_edge[...] = jnp.concatenate(
        [jnp.concatenate([edge_half, nil], axis=1), jnp.concatenate([nil, edge_half], axis=1)], axis=0
    ).astype(bf16)
    alive = lax.broadcasted_iota(jnp.int32, (senders, width), 0) < counts_ref[0]
    masked[...] = jnp.where(alive, 0.5 * b_edge[...], -1e30).astype(bf16)

    @pl.loop(0, slots // GROUP)
    def _(group):
        base = pl.multiple_of(group * GROUP, GROUP)
        own_rows = recv_half[pl.ds(base, GROUP), :].astype(bf16)
        near = scaled[pl.ds(base, GROUP), :].astype(bf16)
        sums = []
        for i in range(0, GROUP, 2 * PAIRS):
            edges = []
            for p in range(PAIRS):
                halves = []
                for n in (i + 2 * p, i + 2 * p + 1):
                    s = jnp.concatenate(
                        [
                            jnp.transpose(jnp.broadcast_to(near[n : n + 1, b : b + slots], (width, slots)))
                            for b in range(0, senders, slots)
                        ],
                        axis=0,
                    )
                    pre = (own_rows[n : n + 1] + send_half[...]) + s * rel_half
                    halves.append(pre * (jnp.tanh(pre) + 1))
                edges.append(jnp.concatenate(halves, axis=1))
            msgs = jnp.dot(
                jnp.concatenate(edges, axis=0), pair_edge[...], preferred_element_type=f32
            ).astype(bf16)
            for n in range(2 * PAIRS):
                p, h = divmod(n, 2)
                msg = msgs[p * senders : (p + 1) * senders, h * width : (h + 1) * width]
                msg = msg + masked[...]
                msg = msg * (jnp.tanh(msg) + 1)
                total = jnp.zeros((8, width), f32)
                for b in range(0, senders, slots):
                    parts = [msg[r : r + PACK] for r in range(b, b + slots, PACK)]
                    while len(parts) > 1:
                        parts = [v + w for v, w in zip(parts[::2], parts[1::2])]
                    part = parts[0].astype(f32)
                    total = total + (part[:8] + part[8:])
                sums.append(jnp.sum(total, axis=0, keepdims=True))
        pooled[pl.ds(base, GROUP), :] = jnp.concatenate(sums, axis=0)

    mean = (pooled[...] / slots).astype(bf16)
    hidden = jax.nn.silu(
        jnp.dot(latent, w_self[0], preferred_element_type=f32)
        + jnp.dot(mean, w_agg[0], preferred_element_type=f32)
    ).astype(bf16)
    result = jnp.dot(hidden, w_out[0], preferred_element_type=f32)
    center = jnp.mean(result, axis=-1, keepdims=True)
    shifted = result - center
    spread = jnp.mean(shifted * shifted, axis=-1, keepdims=True)
    normed = shifted * lax.rsqrt(spread + 1e-05) * norm_gain[...]
    out_ref[0, 0, 0] = (latent.astype(f32) + normed).astype(bf16)

    for (when, copy, _, _), (relay, _, _) in zip(sends, relays):

        def finish(copy=copy, relay=relay):
            copy.wait_send()
            if has_mate:
                relay.wait_send()

        guarded(when, finish)
    if has_mate:
        mate_copy.wait_send()


def shards(latents, offsets, neighbours, counts, *weights):
    slots, width = latents.shape[3:]
    senders = neighbours.shape[3]
    count = slots_of("gx") * slots_of("gy") * slots_of("gz")
    routes = 9
    f32, bf16 = jnp.float32, jnp.bfloat16
    vmem = pl.BlockSpec(memory_space=pltpu.VMEM)
    args = (counts, latents, offsets, neighbours) + weights
    return pl.pallas_call(
        kernel,
        out_shape=jax.ShapeDtypeStruct(latents.shape, latents.dtype),
        in_specs=[pl.BlockSpec(memory_space=pl.ANY)] * INPUTS,
        out_specs=vmem,
        scratch_shapes=[pltpu.VMEM(a.shape, a.dtype) for a in args]
        + [
            pltpu.SemaphoreType.DMA((INPUTS,)),
            pltpu.VMEM((count, slots + PACK, width), bf16),
            pltpu.VMEM((slots, width), f32),
            pltpu.VMEM((senders, width), bf16),
            pltpu.VMEM((slots, senders), f32),
            pltpu.VMEM((slots, width), f32),
            pltpu.VMEM((2 * width, 2 * width), bf16),
            pltpu.VMEM((senders, width), bf16),
            pltpu.VMEM((count // slots_of("gz"), senders, slots * slots_of("gz")), bf16),
            pltpu.SemaphoreType.DMA((routes,)),
            pltpu.SemaphoreType.DMA((count,)),
            pltpu.SemaphoreType.DMA((routes,)),
        ],
        compiler_params=pltpu.CompilerParams(collective_id=0, has_side_effects=True),
    )(*args)


def solution(mesh):
    cells = ("groups", "gx"), "gy", "gz"
    in_specs = (P(*cells, None, None), P(*cells, None, None), P(*cells, None), P(*cells))
    in_specs += (P(),) * 10
    return jax.shard_map(
        shards, mesh=mesh, in_specs=in_specs, out_specs=P(*cells, None, None), check_vma=False
    )
```

profile of v0, /device:TPU:0, one launch (start us, length us, event | category | flops | bytes accessed | tf_op | source)
XLA Modules:
  0.0 20.8 jit_solution(9427633156781216070)
XLA Ops:
  0.7 18.7 %shard_map.136 = bf16[1,1,1,128,128]{4,3,2,1,0:T(8,128)(2,1)} custom-call(s32[1,1,1]{2,1,0:T(1,128)S(6)} %copy.16.refs_0_, bf16[1,1,1,128,128]{4,3,2,1,0:T(8,128)(2,1)} %refs_1_.1, bf16[1,1,1,3,128]{4,3,2,1,0:T(4,128)(2,1)} %refs_2_.1, s32[1,1,1,384]{3,2,1,0:T(1,128)} %refs_3_.1, bf16[1,128,128]{2,1,0:T(8,128)(2,1)} %refs_4_.1, ...), custom_call_target="tpu_custom_call" | custom-call | tf_op jit(solution)/shard_map/pallas_call | solution.py:344
  19.4 1.4 %copy.17 = bf16[1,1,1,128,128]{4,3,2,1,0:T(8,128)(2,1)} copy(bf16[1,1,1,128,128]{4,3,2,1,0:T(8,128)(2,1)} %shard_map.136) | data formatting | bytes 65536
where the time goes:
time: 21.1 us; the launch traced here: 20.8 us
  Pallas kernels  18.7 us (89%)
  local copies, waits for them, and re-layouts  1.38 us (7%)
  between operations  0.66 us (3%)
    pallas_call x1, Pallas kernels, shards(): pl.pallas_call(kernel, out_shape=jax.ShapeDtypeStruct(latents.shape, late...  18.7 us
    unnamed x1, local copies, waits for them, and re-layouts  1.38 us

commit v1 on v0

v1 whole, which is shorter than its diff:
```python
import functools

import jax
import jax.numpy as jnp
from jax import lax
from jax.experimental import pallas as pl
from jax.experimental.pallas import tpu as pltpu
from jax.sharding import PartitionSpec as P

MESH = pl.DeviceIdType.MESH
AXES = ("gx", "gy", "gz")
PACK = 16
EARLY_GROUP = 16
GROUP = 32
NT = (((1,), (1,)), ((), ()))
f32, bf16 = jnp.float32, jnp.bfloat16


def split(value, size):
    if size & (size - 1) == 0:
        return value >> (size.bit_length() - 1), value & (size - 1)
    return lax.div(value, size), lax.rem(value, size)


def wide(axis):
    return lax.axis_size(axis) > 2


def slots_of(axis):
    return min(lax.axis_size(axis), 3)


def moves(axis):
    size, here = lax.axis_size(axis), lax.axis_index(axis)
    if size == 1:
        return []
    if size == 2:
        return [(1 - here, None)]
    return [(here - 1, here > 0), (here + 1, here < size - 1)]


def slot_on(axis, source, target):
    return source - target + 1 if wide(axis) else source


def both(*conditions):
    held = [c for c in conditions if c is not None]
    return functools.reduce(jnp.logical_and, held) if held else None


def guarded(condition, action):
    if condition is None:
        action()
    else:
        pl.when(condition)(action)


def dot(a, b):
    return jnp.dot(a, b, preferred_element_type=f32)


def dot_nt(a, b):
    return lax.dot_general(a, b, NT, preferred_element_type=f32)


def edges_of(own, near, send, rel_half):
    halves = []
    for n in range(2):
        gap = jnp.transpose(jnp.broadcast_to(near[n : n + 1], (send.shape[1], send.shape[0])))
        pre = (own[n : n + 1] + send) + gap * rel_half
        halves.append(pre * (jnp.tanh(pre) + 1))
    return jnp.concatenate(halves, axis=1)


def messages_of(result, masked):
    width = masked.shape[1]
    half, sums = result.astype(bf16), []
    for n in range(2):
        total = None
        for r in range(0, masked.shape[0], PACK):
            msg = half[r : r + PACK, n * width : (n + 1) * width] + masked[r : r + PACK]
            gate = jnp.tanh(msg) + 1
            term = msg.astype(f32) * gate.astype(f32)
            total = term if total is None else total + term
        sums.append(total[:8] + total[8:])
    return sums


def fold_rows(part, rows):
    total = part[pl.ds(0, rows, stride=8), :]
    for k in range(1, 8):
        total = total + part[pl.ds(k, rows, stride=8), :]
    return total


A_INPUTS = 10
A_OUTPUTS = 7
LOAD_ORDER = (1, 5, 2, 6, 3, 0, 4, 7, 8, 9)


def exchange(*refs):
    hbm, outs = refs[:A_INPUTS], refs[A_INPUTS : A_INPUTS + A_OUTPUTS]
    held = refs[A_INPUTS + A_OUTPUTS : 2 * A_INPUTS + A_OUTPUTS]
    load_sem, table, chosen, part, send_sem, recv_sem = refs[2 * A_INPUTS + A_OUTPUTS :]
    counts_ref, latents_ref, offsets_ref, neighbours_ref, w_recv, w_send, w_rel, b_first, w_edge, b_edge = held
    send_half, near, recv_half, masked, pair_edge, pooled, tally = outs
    loads = [pltpu.make_async_copy(src, dst, load_sem.at[n]) for n, (src, dst) in enumerate(zip(hbm, held))]
    for n in LOAD_ORDER:
        loads[n].start()
    slots, width = latents_ref.shape[3], latents_ref.shape[4]
    senders = neighbours_ref.shape[3]
    blocks, room = senders // slots, senders + slots
    here = [lax.axis_index(axis) for axis in AXES]
    sizes = [lax.axis_size(axis) for axis in AXES]
    spans = [slots_of(axis) for axis in AXES]
    count, span_z = table.shape[0], spans[2]

    def slot(coords):
        return (coords[0] * spans[1] + coords[1]) * spans[2] + coords[2]

    def slot_between(source, target):
        return slot([slot_on(a, s, t) for a, s, t in zip(AXES, source, target)])

    own = slot_between(here, here)
    choices = [[(h, None, 0)] + [(v, when, 1) for v, when in moves(a)] for a, h in zip(AXES, here)]
    routes = []
    for x, when_x, far_x in choices[0]:
        for y, when_y, far_y in choices[1]:
            for z, when_z, far_z in choices[2]:
                if far_x + far_y + far_z:
                    routes.append((far_x + far_y, far_z, (x, y, z), both(when_x, when_y, when_z)))
    routes.sort(key=lambda r: (r[0] > 0, r[0]))

    def device(there):
        return dict(zip(AXES, there))

    barrier = pltpu.get_barrier_semaphore()

    def hello(there):
        pl.semaphore_signal(barrier, inc=1, device_id=device(there), device_id_type=MESH)

    for _, _, there, when in routes:
        guarded(when, functools.partial(hello, there))

    for n in (1, 5, 2, 6):
        loads[n].wait()
    latent = latents_ref[0, 0, 0]
    place = offsets_ref[0, 0, 0].astype(f32)
    rel = w_rel[0].astype(f32)
    rows = lax.broadcasted_iota(jnp.int32, (PACK, slots), 0)
    extra = jnp.zeros((PACK, slots), f32)
    for c in range(3):
        extra = jnp.where(rows == c, place[c : c + 1, :], extra)
        extra = jnp.where(rows == 3 + c, here[c].astype(f32), extra)
    col_ids = lax.broadcasted_iota(jnp.int32, (slots, slots), 0)
    spread = jnp.zeros((slots, slots), f32)
    rel_rows = jnp.zeros((slots, width), f32)
    for c in range(3):
        spread = jnp.where(col_ids == c, place[c : c + 1, :], spread)
        rel_rows = jnp.where(col_ids == c, rel[c : c + 1, :], rel_rows)
    rel_rows = rel_rows.astype(bf16)
    shift = dot(jnp.transpose(spread).astype(bf16), rel_rows)
    table[own, :slots, :] = (dot(latent, w_send[0]) + shift).astype(bf16)
    table[own, slots:, :] = extra.astype(bf16)

    peers = jnp.int32(0)
    for _, _, _, when in routes:
        peers = peers + (1 if when is None else when.astype(jnp.int32))
    pl.semaphore_wait(barrier, peers)

    sends = []
    for n, (_, far_z, there, when) in enumerate(routes):
        mine = slot_between(there, here)
        copy, arrival = [
            pltpu.make_async_remote_copy(
                src_ref=table.at[own], dst_ref=table.at[spot], send_sem=send_sem.at[n],
                recv_sem=recv_sem.at[spot], device_id=device(there), device_id_type=MESH,
            )
            for spot in (slot_between(here, there), mine)
        ]
        sends.append((when, copy, arrival, mine))
    for when, copy, _, _ in sends:
        guarded(when, copy.start)

    def clear(which):
        table[which] = jnp.zeros(table.shape[1:], bf16)

    for when, _, _, mine in sends:
        if when is not None:
            pl.when(jnp.logical_not(when))(functools.partial(clear, mine))

    for n in (3, 0, 4, 7, 8, 9):
        loads[n].wait()
    ids = jnp.concatenate([neighbours_ref[0, 0][:, b * slots : (b + 1) * slots] for b in range(blocks)], axis=0)
    cell, at = split(ids, slots)
    cell, z = split(cell, sizes[2])
    x, y = split(cell, sizes[1])
    found = [v - h + 1 if wide(a) else v for a, v, h in zip(AXES, (x, y, z), here)]
    spot = slot(found)
    index = lax.broadcasted_iota(jnp.int32, (blocks, slots), 0) * slots
    index = index + lax.broadcasted_iota(jnp.int32, (blocks, slots), 1)
    live = index < counts_ref[0]
    own_line = own // span_z
    near_by = jnp.logical_and(spot >= own_line * span_z, spot < (own_line + 1) * span_z)
    early = jnp.where(jnp.logical_and(live, near_by), 1.0, 0.0)
    late = jnp.where(live, 1.0, 0.0) - early
    marks = jnp.concatenate([early, late, jnp.zeros((PACK - 2 * blocks, slots), f32)], axis=0).astype(bf16)
    a = lax.broadcasted_iota(jnp.int32, (slots, slots), 0)
    b = lax.broadcasted_iota(jnp.int32, (slots, slots), 1)
    ahead = jnp.concatenate([jnp.where(a < b, 1.0, 0.0), jnp.ones((slots, slots), f32)], axis=1).astype(bf16)
    ranks = dot(marks, ahead)
    rank, whole = ranks[:, :slots], ranks[:, slots:]
    n_early = sum(whole[b : b + 1] for b in range(blocks))
    n_late = sum(whole[blocks + b : blocks + b + 1] for b in range(blocks))
    start = jnp.maximum(n_early, float(slots))
    tally[...] = jnp.broadcast_to(start + n_late - float(slots), tally.shape)
    order = lax.broadcasted_iota(jnp.int32, (room, slots), 0).astype(f32)
    picks, high, low = [], [], []
    base_early, base_late = jnp.zeros((1, slots), f32), start
    for b in range(blocks):
        first = jnp.where(early[b : b + 1] > 0, rank[b : b + 1] + base_early, -1.0)
        goal = jnp.where(late[b : b + 1] > 0, rank[blocks + b : blocks + b + 1] + base_late, first)
        base_early = base_early + whole[b : b + 1]
        base_late = base_late + whole[blocks + b : blocks + b + 1]
        picks.append(jnp.where(order == goal, 1.0, 0.0).astype(bf16))
        high.append((spot[b : b + 1] * slots).astype(f32))
        low.append((at[b : b + 1] + 1).astype(f32))
    picks = jnp.concatenate(picks, axis=1)
    high = jnp.broadcast_to(jnp.concatenate(high, axis=1), (slots, senders)).astype(bf16)
    low = jnp.broadcast_to(jnp.concatenate(low, axis=1), (slots, senders)).astype(bf16)
    sorted_ids = dot_nt(picks, high) + dot_nt(picks, low)
    masked[...] = jnp.where(sorted_ids > 0.5, 0.5 * b_edge[...], -1e30).astype(bf16)
    sorted_ids = sorted_ids.astype(jnp.int32) - 1
    lanes = lax.broadcasted_iota(jnp.int32, (room, slots), 1)

    cell_x, cell_z = split(a, spans[2])
    cell_x, cell_y = split(cell_x, spans[1])
    step = jnp.zeros((slots, width), f32)
    for c, v in enumerate((cell_x, cell_y, cell_z)):
        gap = v - 1 if wide(AXES[c]) else v - here[c]
        step = step + gap.astype(f32) * rel[c : c + 1]
    step_high = step.astype(bf16)
    step_low = (step - step_high.astype(f32)).astype(bf16)
    of_cell = jnp.where(lax.shift_right_arithmetic(sorted_ids, slots.bit_length() - 1) == lanes, 1.0, 0.0).astype(bf16)
    moved = dot(of_cell, step_high) + dot(of_cell, step_low)

    def choose(line):
        for k in range(span_z):
            hit = sorted_ids - (line * span_z + k) * slots == lanes
            chosen[line, :, k * slots : (k + 1) * slots] = jnp.where(hit, 1.0, 0.0).astype(bf16)

    for line in range(count // span_z):
        choose(line)

    edge_half = 0.5 * w_edge[0].astype(f32)
    nil = jnp.zeros_like(edge_half)
    pair_edge[...] = jnp.concatenate(
        [jnp.concatenate([edge_half, nil], axis=1), jnp.concatenate([nil, edge_half], axis=1)], axis=0
    ).astype(bf16)
    rel_half = (0.5 * rel[3:4]).astype(bf16)
    recv_half[...] = 0.5 * (dot(latent, w_recv[0]) + b_first[...] - shift)
    place_cols = [jnp.transpose(jnp.broadcast_to(place[c : c + 1], (slots, slots))) for c in range(3)]

    def gather(line, top, bottom):
        picked, cells = chosen[line, top:bottom, :], table.at[pl.ds(line * span_z, span_z)]
        rows_of = cells[:, :slots, :].reshape(span_z * slots, width)
        extras = cells[:, slots:, :]
        extras = jnp.concatenate([extras[k] for k in range(span_z)], axis=1)
        return dot(picked, rows_of), dot_nt(extras, picked)

    def place_block(b, feats):
        square = jnp.zeros((slots, slots), f32)
        for c in range(3):
            where = feats[c : c + 1] + (feats[3 + c : 4 + c] - here[c].astype(f32))
            apart = where - place_cols[c]
            square = square + apart * apart
        near[b] = 0.25 * square

    for (far, far_z, _, when), (_, _, arrival, _) in zip(routes, sends):
        if far == 0:
            guarded(when, arrival.wait_recv)
    rows_of, feats = gather(own_line, 0, room)
    send_half[:slots, :] = (0.5 * (rows_of[:slots] + moved[:slots])).astype(bf16)
    place_block(0, feats[:, :slots])
    carry = (rows_of[slots:] + moved[slots:], feats[:, slots:])

    @pl.loop(0, slots // EARLY_GROUP)
    def _(group):
        base = pl.multiple_of(group * EARLY_GROUP, EARLY_GROUP)
        own_rows = recv_half[pl.ds(base, EARLY_GROUP), :].astype(bf16)
        near_rows = near[0, pl.ds(base, EARLY_GROUP), :].astype(bf16)
        for i in range(0, EARLY_GROUP, 2):
            edges = edges_of(own_rows[i : i + 2], near_rows[i : i + 2], send_half[:slots, :], rel_half)
            sums = messages_of(dot(edges, pair_edge[...]), masked[:slots, :])
            for n in range(2):
                part[pl.ds(pl.multiple_of((base + i + n) * 8, 8), 8), :] = sums[n]

    pooled[...] = fold_rows(part, slots)

    pairs = {}
    for (far, far_z, there, when), (_, _, arrival, mine) in zip(routes, sends):
        if far:
            guarded(when, arrival.wait_recv)
            pairs.setdefault((id(there[0]), id(there[1])), []).append(mine)
            if len(pairs[id(there[0]), id(there[1])]) == span_z:
                rows_of, feats = gather(mine // span_z, slots, room)
                carry = (carry[0] + rows_of, carry[1] + feats)
    send_half[slots:, :] = (0.5 * carry[0]).astype(bf16)
    for b in range(blocks):
        place_block(b + 1, carry[1][:, b * slots : (b + 1) * slots])

    for when, copy, _, _ in sends:
        guarded(when, copy.wait_send)


B_LOADS = 6


def finish(*refs):
    send_half, near, recv_half, masked, pair_edge, pooled, tally = refs[:7]
    hbm, out_ref = refs[7 : 7 + B_LOADS], refs[7 + B_LOADS]
    held = refs[8 + B_LOADS : 8 + 2 * B_LOADS]
    load_sem, part = refs[8 + 2 * B_LOADS :]
    latents_ref, w_rel, w_self, w_agg, w_out, norm_gain = held
    loads = [pltpu.make_async_copy(src, dst, load_sem.at[n]) for n, (src, dst) in enumerate(zip(hbm, held))]
    for n in (1, 0, 2, 3, 4, 5):
        loads[n].start()
    slots, width = recv_half.shape
    used = jnp.max(tally[...]).astype(jnp.int32)
    steps = lax.div(used + (slots - 1), jnp.int32(slots)) * (slots // GROUP)
    part[...] = jnp.zeros_like(part)
    loads[1].wait()
    rel_half = (0.5 * w_rel[0][3:4].astype(f32)).astype(bf16)

    @pl.loop(0, steps)
    def _(step):
        block, group = split(step, slots // GROUP)
        block = block + 1
        top = pl.multiple_of(block * slots, slots)
        base = pl.multiple_of(group * GROUP, GROUP)
        own_rows = recv_half[pl.ds(base, GROUP), :].astype(bf16)
        near_rows = near[block, pl.ds(base, GROUP), :].astype(bf16)
        for i in range(0, GROUP, 2):
            edges = edges_of(own_rows[i : i + 2], near_rows[i : i + 2], send_half[pl.ds(top, slots), :], rel_half)
            sums = messages_of(dot(edges, pair_edge[...]), masked[pl.ds(top, slots), :])
            for n in range(2):
                spot = pl.ds(pl.multiple_of((base + i + n) * 8, 8), 8)
                part[spot, :] = part[spot, :] + sums[n]

    for n in (0, 2, 3, 4, 5):
        loads[n].wait()
    latent = latents_ref[0, 0, 0]
    mean = ((pooled[...] + fold_rows(part, slots)) / slots).astype(bf16)
    hidden = jax.nn.silu(dot(latent, w_self[0]) + dot(mean, w_agg[0])).astype(bf16)
    result = dot(hidden, w_out[0])
    center = jnp.mean(result, axis=-1, keepdims=True)
    shifted = result - center
    spread = jnp.mean(shifted * shifted, axis=-1, keepdims=True)
    normed = shifted * lax.rsqrt(spread + 1e-05) * norm_gain[...]
    out_ref[0, 0, 0] = (latent.astype(f32) + normed).astype(bf16)


def pinned(value):
    return pltpu.with_memory_space_constraint(value, pltpu.HBM)


def shards(
    latents, offsets, neighbours, counts, w_recv, w_send, w_rel, b_first, w_edge, b_edge, w_self, w_agg, w_out, norm_gain
):
    slots, width = latents.shape[3:]
    senders = neighbours.shape[3]
    room = senders + slots
    spans = [slots_of(axis) for axis in AXES]
    count = spans[0] * spans[1] * spans[2]
    vmem = pl.BlockSpec(memory_space=pltpu.VMEM)
    far = pl.BlockSpec(memory_space=pltpu.HBM)
    args = (counts, latents, offsets, neighbours, w_recv, w_send, w_rel, b_first, w_edge, b_edge)
    between = (
        ((room, width), bf16), ((room // slots, slots, slots), f32), ((slots, width), f32), ((room, width), bf16),
        ((2 * width, 2 * width), bf16), ((slots, width), f32), ((8, slots), f32),
    )
    found = pl.pallas_call(
        exchange,
        out_shape=[jax.ShapeDtypeStruct(*s) for s in between],
        in_specs=[far] * A_INPUTS,
        out_specs=[vmem] * A_OUTPUTS,
        scratch_shapes=[pltpu.VMEM(v.shape, v.dtype) for v in args]
        + [
            pltpu.SemaphoreType.DMA((A_INPUTS,)),
            pltpu.VMEM((count, slots + PACK, width), bf16),
            pltpu.VMEM((count // spans[2], room, slots * spans[2]), bf16),
            pltpu.VMEM((slots * 8, width), f32),
            pltpu.SemaphoreType.DMA((27,)),
            pltpu.SemaphoreType.DMA((count,)),
        ],
        compiler_params=pltpu.CompilerParams(
            collective_id=0, has_side_effects=True, vmem_limit_bytes=24 * 1024 * 1024
        ),
    )(args[0], *[pinned(v) for v in args[1:]])
    rest = tuple(pinned(v) for v in (latents, w_rel, w_self, w_agg, w_out, norm_gain))
    return pl.pallas_call(
        finish,
        out_shape=jax.ShapeDtypeStruct(latents.shape, latents.dtype),
        in_specs=[vmem] * A_OUTPUTS + [far] * B_LOADS,
        out_specs=vmem,
        scratch_shapes=[pltpu.VMEM(v.shape, v.dtype) for v in rest]
        + [pltpu.SemaphoreType.DMA((B_LOADS,)), pltpu.VMEM((slots * 8, width), f32)],
        compiler_params=pltpu.CompilerParams(vmem_limit_bytes=24 * 1024 * 1024),
    )(*found, *rest)


def solution(mesh):
    cells = ("groups", "gx"), "gy", "gz"
    in_specs = (P(*cells, None, None), P(*cells, None, None), P(*cells, None), P(*cells))
    in_specs += (P(),) * 10
    return jax.shard_map(
        shards, mesh=mesh, in_specs=in_specs, out_specs=P(*cells, None, None), check_vma=False
    )
```

time: 21.1 us -> 18.7 us (0.89)
  local copies, waits for them, and re-layouts: 1.38 us -> 0 us
  Pallas kernels: 18.7 us -> 17.7 us
    unnamed x1 -> x0, local copies, waits for them, and re-layouts: 1.38 us -> none
    pallas_call x1 -> x2, Pallas kernels: 18.7 us -> 17.7 us  [the longest x1 10.1 us: shards(): pl.pallas_call(exchange, out_shape=[jax.ShapeDtypeStruct(*s) for s in bet...]
where the time goes in v1:
time: 18.7 us; the launch traced here: 18.4 us
  Pallas kernels  17.7 us (95%)
  between operations  0.66 us (4%)
    pallas_call x1, Pallas kernels, shards(): pl.pallas_call(exchange, out_shape=[jax.ShapeDtypeStruct(*s) for s in bet...  10.1 us
    pallas_call x1, Pallas kernels, shards(): pl.pallas_call(finish, out_shape=jax.ShapeDtypeStruct(latents.shape, late...  7.63 us

profile of v1, /device:TPU:0, one launch (start us, length us, event | category | flops | bytes accessed | tf_op | source)
XLA Modules:
  0.0 18.4 jit_solution(16570629443913239250)
XLA Ops:
  0.7 10.1 %shard_map.136 = (bf16[512,128]{1,0:T(8,128)(2,1)S(1)}, f32[4,128,128]{2,1,0:T(8,128)S(1)}, f32[128,128]{1,0:T(8,128)S(1)}, bf16[512,128]{1,0:T(8,128)(2,1)S(1)}...) custom-call(s32[1,1,1]{2,1,0:T(1,128)S(6)} %copy.15.refs_0_, ...), custom_call_target="tpu_custom_call" | custom-call | tf_op jit(solution)/shard_map/pallas_call | solution.py:382
  10.8 7.6 %shard_map.137 = bf16[1,1,1,128,128]{4,3,2,1,0:T(8,128)(2,1)} custom-call(bf16[512,128]{1,0:T(8,128)(2,1)S(1)} %get-tuple-element.12.refs_0_, f32[4,128,128]{2,1,0:T(8,128)S(1)} %get-tuple-element.13.refs_1_, f32[128,128]{1,0:T(8,128)S(1)} %get-tuple-element.14.refs_2_, bf16[512,128]{1,0:T(8,128)(2,1)S(1)} %get-tuple-element.15.refs_3_, ...), custom_call_target="tpu_custom_call" | custom-call | tf_op jit(solution)/shard_map/pallas_call | solution.py:401

commit v2 on v1

v2 whole, which is shorter than its diff:
```python
import functools

import jax
import jax.numpy as jnp
from jax import lax
from jax.experimental import pallas as pl
from jax.experimental.pallas import tpu as pltpu
from jax.sharding import PartitionSpec as P

MESH = pl.DeviceIdType.MESH
AXES = ("gx", "gy", "gz")
PACK = 16
GROUP = 64
CLASSES = 3
RELAYED = 2
NT = (((1,), (1,)), ((), ()))
f32, bf16 = jnp.float32, jnp.bfloat16


def split(value, size):
    if size & (size - 1) == 0:
        return value >> (size.bit_length() - 1), value & (size - 1)
    return lax.div(value, size), lax.rem(value, size)


def wide(axis):
    return lax.axis_size(axis) > 2


def slots_of(axis):
    return min(lax.axis_size(axis), 3)


def moves(axis):
    size, here = lax.axis_size(axis), lax.axis_index(axis)
    if size == 1:
        return []
    if size == 2:
        return [(1 - here, None)]
    return [(here - 1, here > 0), (here + 1, here < size - 1)]


def slot_on(axis, source, target):
    return source - target + 1 if wide(axis) else source


def both(*conditions):
    held = [c for c in conditions if c is not None]
    return functools.reduce(jnp.logical_and, held) if held else None


def guarded(condition, action):
    if condition is None:
        action()
    else:
        pl.when(condition)(action)


def dot(a, b):
    return jnp.dot(a, b, preferred_element_type=f32)


def dot_nt(a, b):
    return lax.dot_general(a, b, NT, preferred_element_type=f32)


def edges_of(own, near, send, rel_half):
    halves = []
    for n in range(2):
        gap = jnp.transpose(jnp.broadcast_to(near[n : n + 1], (send.shape[1], send.shape[0])))
        pre = (own[n : n + 1] + send) + gap * rel_half
        halves.append(pre * (jnp.tanh(pre) + 1))
    return jnp.concatenate(halves, axis=1)


def messages_of(result, masked):
    width = masked.shape[1]
    half, sums = result.astype(bf16), []
    for n in range(2):
        total = None
        for r in range(0, masked.shape[0], PACK):
            msg = half[r : r + PACK, n * width : (n + 1) * width] + masked[r : r + PACK]
            gate = jnp.tanh(msg) + 1
            term = msg.astype(f32) * gate.astype(f32)
            total = term if total is None else total + term
        sums.append(total[:8] + total[8:])
    return sums


def fold_rows(part, rows):
    total = part[pl.ds(0, rows, stride=8), :]
    for k in range(1, 8):
        total = total + part[pl.ds(k, rows, stride=8), :]
    return total


A_INPUTS = 10
A_OUTPUTS = 7
LOAD_ORDER = (1, 5, 2, 6, 3, 0, 4, 7, 8, 9)


def exchange(*refs):
    hbm, outs = refs[:A_INPUTS], refs[A_INPUTS : A_INPUTS + A_OUTPUTS]
    held = refs[A_INPUTS + A_OUTPUTS : 2 * A_INPUTS + A_OUTPUTS]
    load_sem, table, chosen, part, send_sem, relay_sem, recv_sem = refs[2 * A_INPUTS + A_OUTPUTS :]
    counts_ref, latents_ref, offsets_ref, neighbours_ref, w_recv, w_send, w_rel, b_first, w_edge, b_edge = held
    send_half, near, recv_half, masked, pair_edge, pooled, tally = outs
    loads = [pltpu.make_async_copy(src, dst, load_sem.at[n]) for n, (src, dst) in enumerate(zip(hbm, held))]
    for n in LOAD_ORDER:
        loads[n].start()
    slots, width = latents_ref.shape[3], latents_ref.shape[4]
    senders = neighbours_ref.shape[3]
    blocks, room = senders // slots, senders + (CLASSES - 1) * slots
    here = [lax.axis_index(axis) for axis in AXES]
    sizes = [lax.axis_size(axis) for axis in AXES]
    spans = [slots_of(axis) for axis in AXES]
    count, span_z = table.shape[0], spans[2]

    def slot(coords):
        return (coords[0] * spans[1] + coords[1]) * spans[2] + coords[2]

    def slot_between(source, target):
        return slot([slot_on(a, s, t) for a, s, t in zip(AXES, source, target)])

    own = slot_between(here, here)
    own_line = own // span_z
    choices = [[(h, None, 0)] + [(v, when, 1) for v, when in moves(a)] for a, h in zip(AXES[:2], here)]
    routes = []
    for x, when_x, far_x in choices[0]:
        for y, when_y, far_y in choices[1]:
            if far_x + far_y:
                routes.append((far_x + far_y, (x, y, here[2]), both(when_x, when_y)))
    routes.sort(key=lambda r: r[0])
    has_mate = sizes[2] > 1
    mate = (here[0], here[1], 1 - here[2])

    def device(there):
        return dict(zip(AXES, there))

    barrier = pltpu.get_barrier_semaphore()

    def hello(there):
        pl.semaphore_signal(barrier, inc=1, device_id=device(there), device_id_type=MESH)

    if has_mate:
        hello(mate)
    for far, there, when in routes:
        guarded(when, functools.partial(hello, there))
        if has_mate and far < RELAYED:
            guarded(when, functools.partial(hello, (there[0], there[1], mate[2])))

    for n in (1, 5, 2, 6):
        loads[n].wait()
    latent = latents_ref[0, 0, 0]
    place = offsets_ref[0, 0, 0].astype(f32)
    rel = w_rel[0].astype(f32)
    rows = lax.broadcasted_iota(jnp.int32, (PACK, slots), 0)
    extra = jnp.zeros((PACK, slots), f32)
    for c in range(3):
        extra = jnp.where(rows == c, place[c : c + 1, :], extra)
        extra = jnp.where(rows == 3 + c, here[c].astype(f32), extra)
    col_ids = lax.broadcasted_iota(jnp.int32, (slots, slots), 0)
    spread = jnp.zeros((slots, slots), f32)
    rel_rows = jnp.zeros((slots, width), f32)
    for c in range(3):
        spread = jnp.where(col_ids == c, place[c : c + 1, :], spread)
        rel_rows = jnp.where(col_ids == c, rel[c : c + 1, :], rel_rows)
    rel_rows = rel_rows.astype(bf16)
    shift = dot(jnp.transpose(spread).astype(bf16), rel_rows)
    table[own, :slots, :] = (dot(latent, w_send[0]) + shift).astype(bf16)
    table[own, slots:, :] = extra.astype(bf16)

    for n in (3, 0):
        loads[n].wait()
    ids = jnp.concatenate([neighbours_ref[0, 0][:, b * slots : (b + 1) * slots] for b in range(blocks)], axis=0)
    cell, at = split(ids, slots)
    cell, z = split(cell, sizes[2])
    x, y = split(cell, sizes[1])
    found = [v - h + 1 if wide(a) else v for a, v, h in zip(AXES, (x, y, z), here)]
    spot = slot(found)
    index = lax.broadcasted_iota(jnp.int32, (blocks, slots), 0) * slots
    index = index + lax.broadcasted_iota(jnp.int32, (blocks, slots), 1)
    live = index < counts_ref[0]
    apart = sum(jnp.where(found[c] == slot_on(AXES[c], here[c], here[c]), 0, 1) for c in range(2))
    classes = [jnp.where(jnp.logical_and(live, apart == k), 1.0, 0.0) for k in range(CLASSES)]
    spare = -(CLASSES * blocks) % PACK
    marks = jnp.concatenate(classes + [jnp.zeros((spare, slots), f32)], axis=0).astype(bf16)
    a = lax.broadcasted_iota(jnp.int32, (slots, slots), 0)
    b = lax.broadcasted_iota(jnp.int32, (slots, slots), 1)
    ahead = jnp.concatenate([jnp.where(a < b, 1.0, 0.0), jnp.ones((slots, slots), f32)], axis=1).astype(bf16)
    ranks = dot(marks, ahead)
    goals = [jnp.full((1, slots), -1.0, f32)] * blocks
    base = jnp.zeros((1, slots), f32)
    for k in range(CLASSES):
        base = jnp.maximum(base, float(k * slots))
        for b in range(blocks):
            row = slice(k * blocks + b, k * blocks + b + 1)
            goals[b] = jnp.where(classes[k][b : b + 1] > 0, ranks[row, :slots] + base, goals[b])
            base = base + ranks[row, slots:]
    tally[:8, :] = jnp.broadcast_to(base - float((CLASSES - 1) * slots), (8, slots))
    tally[8:, :] = jnp.broadcast_to(0.5 * rel[3:4], (8, width))

    peers = jnp.int32(1 if has_mate else 0)
    for far, _, when in routes:
        cores = 2 if has_mate and far < RELAYED else 1
        peers = peers + (cores if when is None else cores * when.astype(jnp.int32))
    pl.semaphore_wait(barrier, peers)

    def remote(source, spot, sem, there):
        return pltpu.make_async_remote_copy(
            src_ref=table.at[source], dst_ref=table.at[spot], send_sem=sem, recv_sem=recv_sem.at[spot],
            device_id=device(there), device_id_type=MESH,
        )

    lines, sends, relays = [(own_line, 0)], [], []
    for far, there, when in routes:
        mine = slot_between(there, here)
        twin = slot_between((there[0], there[1], mate[2]), here)
        lines.append((mine // span_z, far))
        other = (there[0], there[1], mate[2])
        n = len(sends)
        sends.append((far, when, remote(own, slot_between(here, there), send_sem.at[n], there),
                      remote(own, mine, send_sem.at[n], there), mine))
        if not has_mate:
            continue
        if far < RELAYED:
            sends.append((far, when, remote(own, slot_between(here, other), send_sem.at[n + 1], other),
                          remote(own, twin, send_sem.at[n + 1], other), twin))
        else:
            n = len(relays)
            relays.append((far, when, remote(mine, mine, relay_sem.at[n], mate), sends[-1][3],
                           remote(own, twin, relay_sem.at[n], mate), twin))
    if has_mate:
        mate_own = slot_between(mate, here)
        mate_copy = remote(own, own, send_sem.at[len(sends)], mate)
        mate_in = remote(own, mate_own, send_sem.at[len(sends)], mate)
        mate_copy.start()
    for _, when, copy, _, _ in sends:
        guarded(when, copy.start)

    def clear(which):
        table[which] = jnp.zeros(table.shape[1:], bf16)

    for when, which in [(s[1], s[4]) for s in sends] + [(r[1], r[5]) for r in relays]:
        if when is not None:
            pl.when(jnp.logical_not(when))(functools.partial(clear, which))

    for n in (4, 7, 8, 9):
        loads[n].wait()
    order = lax.broadcasted_iota(jnp.int32, (room, slots), 0).astype(f32)
    picks, high, low = [], [], []
    for b in range(blocks):
        picks.append(jnp.where(order == goals[b], 1.0, 0.0).astype(bf16))
        high.append((spot[b : b + 1] * slots).astype(f32))
        low.append((at[b : b + 1] + 1).astype(f32))
    picks = jnp.concatenate(picks, axis=1)
    high = jnp.broadcast_to(jnp.concatenate(high, axis=1), (slots, senders)).astype(bf16)
    low = jnp.broadcast_to(jnp.concatenate(low, axis=1), (slots, senders)).astype(bf16)
    sorted_ids = dot_nt(picks, high) + dot_nt(picks, low)
    masked[...] = jnp.where(sorted_ids > 0.5, 0.5 * b_edge[...], -1e30).astype(bf16)
    sorted_ids = sorted_ids.astype(jnp.int32) - 1
    lanes = lax.broadcasted_iota(jnp.int32, (room, slots), 1)

    cell_x, cell_z = split(lax.broadcasted_iota(jnp.int32, (slots, slots), 0), spans[2])
    cell_x, cell_y = split(cell_x, spans[1])
    step = jnp.zeros((slots, width), f32)
    for c, v in enumerate((cell_x, cell_y, cell_z)):
        gap = v - 1 if wide(AXES[c]) else v - here[c]
        step = step + gap.astype(f32) * rel[c : c + 1]
    step_high = step.astype(bf16)
    step_low = (step - step_high.astype(f32)).astype(bf16)
    of_cell = jnp.where(lax.shift_right_arithmetic(sorted_ids, slots.bit_length() - 1) == lanes, 1.0, 0.0).astype(bf16)
    moved = dot(of_cell, step_high) + dot(of_cell, step_low)

    for r, (line, far) in enumerate(lines):
        for k in range(span_z):
            hit = sorted_ids[far * slots :] - (line * span_z + k) * slots == lanes[far * slots :]
            chosen[r, far * slots :, k * slots : (k + 1) * slots] = jnp.where(hit, 1.0, 0.0).astype(bf16)

    edge_half = 0.5 * w_edge[0].astype(f32)
    nil = jnp.zeros_like(edge_half)
    pair_edge[...] = jnp.concatenate(
        [jnp.concatenate([edge_half, nil], axis=1), jnp.concatenate([nil, edge_half], axis=1)], axis=0
    ).astype(bf16)
    rel_half = (0.5 * rel[3:4]).astype(bf16)
    recv_half[...] = 0.5 * (dot(latent, w_recv[0]) + b_first[...] - shift)
    place_cols = [jnp.transpose(jnp.broadcast_to(place[c : c + 1], (slots, slots))) for c in range(3)]

    def gather(roles, top, bottom):
        total = moved[top:bottom], jnp.zeros((PACK, bottom - top), f32)
        for r in roles:
            picked, cells = chosen[r, top:bottom, :], table.at[pl.ds(lines[r][0] * span_z, span_z)]
            rows_of = cells[:, :slots, :].reshape(span_z * slots, width)
            extras = cells[:, slots:, :]
            extras = jnp.concatenate([extras[k] for k in range(span_z)], axis=1)
            total = total[0] + dot(picked, rows_of), total[1] + dot_nt(extras, picked)
        send_half[top:bottom, :] = (0.5 * total[0]).astype(bf16)
        for n in range(top // slots, bottom // slots):
            feats = total[1][:, n * slots - top : (n + 1) * slots - top]
            square = jnp.zeros((slots, slots), f32)
            for c in range(3):
                where = feats[c : c + 1] + (feats[3 + c : 4 + c] - here[c].astype(f32))
                gap = where - place_cols[c]
                square = square + gap * gap
            near[n] = 0.25 * square

    def pass_on():
        for _, when, relay, arrival, _, _ in relays:

            def forward(arrival=arrival, relay=relay):
                arrival.wait_recv()
                relay.start()

            guarded(when, forward)

    def work(block):
        top = block * slots

        @pl.loop(0, slots // GROUP)
        def _(group):
            base = pl.multiple_of(group * GROUP, GROUP)
            own_rows = recv_half[pl.ds(base, GROUP), :].astype(bf16)
            near_rows = near[block, pl.ds(base, GROUP), :].astype(bf16)
            for i in range(0, GROUP, 2):
                edges = edges_of(own_rows[i : i + 2], near_rows[i : i + 2], send_half[top : top + slots, :], rel_half)
                sums = messages_of(dot(edges, pair_edge[...]), masked[top : top + slots, :])
                for n in range(2):
                    eight = pl.ds(pl.multiple_of((base + i + n) * 8, 8), 8)
                    part[eight, :] = part[eight, :] + sums[n] if block else sums[n]

            if block + 1 == RELAYED:
                pl.when(group == 0)(pass_on)

    for far in range(CLASSES):
        if has_mate and far == 0:
            mate_in.wait_recv()
        for step_far, when, _, arrival, _ in sends:
            if step_far == far and not (has_mate and far >= RELAYED):
                guarded(when, arrival.wait_recv)
        for step_far, when, _, _, twin_in, _ in relays:
            if step_far == far:
                guarded(when, twin_in.wait_recv)
        roles = [r for r, (_, step_far) in enumerate(lines) if step_far <= far]
        gather(roles, far * slots, room if far == CLASSES - 1 else (far + 1) * slots)
        if far < CLASSES - 1:
            work(far)
        if far == CLASSES - 2:
            pooled[...] = fold_rows(part, slots)

    for when, copy in [(s[1], s[2]) for s in sends] + [(r[1], r[2]) for r in relays]:
        guarded(when, copy.wait_send)
    if has_mate:
        mate_copy.wait_send()


B_LOADS = 5


def finish(*refs):
    send_half, near, recv_half, masked, pair_edge, pooled, tally = refs[:7]
    hbm, out_ref = refs[7 : 7 + B_LOADS], refs[7 + B_LOADS]
    held = refs[8 + B_LOADS : 8 + 2 * B_LOADS]
    load_sem, part = refs[8 + 2 * B_LOADS :]
    latents_ref, w_self, w_agg, w_out, norm_gain = held
    loads = [pltpu.make_async_copy(src, dst, load_sem.at[n]) for n, (src, dst) in enumerate(zip(hbm, held))]
    for load in loads:
        load.start()
    slots, width = recv_half.shape
    used = jnp.max(tally[:8, :]).astype(jnp.int32)
    steps = lax.div(used + (slots - 1), jnp.int32(slots)) * (slots // GROUP)
    part[...] = jnp.zeros_like(part)
    rel_half = tally[8:9, :].astype(bf16)

    @pl.loop(0, steps)
    def _(step):
        block, group = split(step, slots // GROUP)
        block = block + (CLASSES - 1)
        top = pl.multiple_of(block * slots, slots)
        base = pl.multiple_of(group * GROUP, GROUP)
        own_rows = recv_half[pl.ds(base, GROUP), :].astype(bf16)
        near_rows = near[block, pl.ds(base, GROUP), :].astype(bf16)
        for i in range(0, GROUP, 2):
            edges = edges_of(own_rows[i : i + 2], near_rows[i : i + 2], send_half[pl.ds(top, slots), :], rel_half)
            sums = messages_of(dot(edges, pair_edge[...]), masked[pl.ds(top, slots), :])
            for n in range(2):
                spot = pl.ds(pl.multiple_of((base + i + n) * 8, 8), 8)
                part[spot, :] = part[spot, :] + sums[n]

    for load in loads:
        load.wait()
    latent = latents_ref[0, 0, 0]
    mean = ((pooled[...] + fold_rows(part, slots)) / slots).astype(bf16)
    hidden = jax.nn.silu(dot(latent, w_self[0]) + dot(mean, w_agg[0])).astype(bf16)
    result = dot(hidden, w_out[0])
    center = jnp.mean(result, axis=-1, keepdims=True)
    shifted = result - center
    spread = jnp.mean(shifted * shifted, axis=-1, keepdims=True)
    normed = shifted * lax.rsqrt(spread + 1e-05) * norm_gain[...]
    out_ref[0, 0, 0] = (latent.astype(f32) + normed).astype(bf16)


def pinned(value):
    return pltpu.with_memory_space_constraint(value, pltpu.HBM)


def shards(
    latents, offsets, neighbours, counts, w_recv, w_send, w_rel, b_first, w_edge, b_edge, w_self, w_agg, w_out, norm_gain
):
    slots, width = latents.shape[3:]
    senders = neighbours.shape[3]
    room = senders + (CLASSES - 1) * slots
    spans = [slots_of(axis) for axis in AXES]
    count = spans[0] * spans[1] * spans[2]
    vmem = pl.BlockSpec(memory_space=pltpu.VMEM)
    far = pl.BlockSpec(memory_space=pltpu.HBM)
    args = (counts, latents, offsets, neighbours, w_recv, w_send, w_rel, b_first, w_edge, b_edge)
    between = (
        ((room, width), bf16), ((room // slots, slots, slots), f32), ((slots, width), f32), ((room, width), bf16),
        ((2 * width, 2 * width), bf16), ((slots, width), f32), ((16, slots), f32),
    )
    found = pl.pallas_call(
        exchange,
        out_shape=[jax.ShapeDtypeStruct(*s) for s in between],
        in_specs=[far] * A_INPUTS,
        out_specs=[vmem] * A_OUTPUTS,
        scratch_shapes=[pltpu.VMEM(v.shape, v.dtype) for v in args]
        + [
            pltpu.SemaphoreType.DMA((A_INPUTS,)),
            pltpu.VMEM((count, slots + PACK, width), bf16),
            pltpu.VMEM((count // spans[2], room, slots * spans[2]), bf16),
            pltpu.VMEM((slots * 8, width), f32),
            pltpu.SemaphoreType.DMA((18,)),
            pltpu.SemaphoreType.DMA((9,)),
            pltpu.SemaphoreType.DMA((count,)),
        ],
        compiler_params=pltpu.CompilerParams(
            collective_id=0, has_side_effects=True, vmem_limit_bytes=24 * 1024 * 1024
        ),
    )(args[0], *[pinned(v) for v in args[1:]])
    rest = tuple(pinned(v) for v in (latents, w_self, w_agg, w_out, norm_gain))
    return pl.pallas_call(
        finish,
        out_shape=jax.ShapeDtypeStruct(latents.shape, latents.dtype),
        in_specs=[vmem] * A_OUTPUTS + [far] * B_LOADS,
        out_specs=vmem,
        scratch_shapes=[pltpu.VMEM(v.shape, v.dtype) for v in rest]
        + [pltpu.SemaphoreType.DMA((B_LOADS,)), pltpu.VMEM((slots * 8, width), f32)],
        compiler_params=pltpu.CompilerParams(vmem_limit_bytes=24 * 1024 * 1024),
    )(*found, *rest)


def solution(mesh):
    cells = ("groups", "gx"), "gy", "gz"
    in_specs = (P(*cells, None, None), P(*cells, None, None), P(*cells, None), P(*cells))
    in_specs += (P(),) * 10
    return jax.shard_map(
        shards, mesh=mesh, in_specs=in_specs, out_specs=P(*cells, None, None), check_vma=False
    )
```

time: 18.7 us -> 16.9 us (0.904)
  Pallas kernels: 17.7 us -> 16.1 us
    pallas_call x1, Pallas kernels: 7.63 us -> 3.92 us  [shards(): pl.pallas_call(finish, out_shape=jax.ShapeDtypeStruct(latents.shape, late...]
    pallas_call x1, Pallas kernels: 10.1 us -> 12.2 us  [shards(): pl.pallas_call(exchange, out_shape=[jax.ShapeDtypeStruct(*s) for s in bet...]
where the time goes in v2:
time: 16.9 us; the launch traced here: 16.7 us
  Pallas kernels  16.1 us (95%)
  between operations  0.66 us (4%)
    pallas_call x1, Pallas kernels, shards(): pl.pallas_call(exchange, out_shape=[jax.ShapeDtypeStruct(*s) for s in bet...  12.2 us
    pallas_call x1, Pallas kernels, shards(): pl.pallas_call(finish, out_shape=jax.ShapeDtypeStruct(latents.shape, late...  3.92 us

profile of v2, /device:TPU:0, one launch (start us, length us, event | category | flops | bytes accessed | tf_op | source)
XLA Modules:
  0.0 16.7 jit_solution(16351473073875422940)
XLA Ops:
  0.7 12.2 %shard_map.136 = (bf16[640,128]{1,0:T(8,128)(2,1)S(1)}, f32[5,128,128]{2,1,0:T(8,128)S(1)}, f32[128,128]{1,0:T(8,128)S(1)}, bf16[640,128]{1,0:T(8,128)(2,1)S(1)}...) custom-call(s32[1,1,1]{2,1,0:T(1,128)S(6)} %copy.15.refs_0_, ...), custom_call_target="tpu_custom_call" | custom-call | tf_op jit(solution)/shard_map/pallas_call | solution.py:421
  12.8 3.9 %shard_map.137 = bf16[1,1,1,128,128]{4,3,2,1,0:T(8,128)(2,1)} custom-call(bf16[640,128]{1,0:T(8,128)(2,1)S(1)} %get-tuple-element.12.refs_0_, f32[5,128,128]{2,1,0:T(8,128)S(1)} %get-tuple-element.13.refs_1_, f32[128,128]{1,0:T(8,128)S(1)} %get-tuple-element.14.refs_2_, bf16[640,128]{1,0:T(8,128)(2,1)S(1)} %get-tuple-element.15.refs_3_, ...), custom_call_target="tpu_custom_call" | custom-call | tf_op jit(solution)/shard_map/pallas_call | solution.py:441

commit v3 on v2

--- a/solution.py
+++ b/solution.py
@@ -200,6 +200,33 @@
     tally[:8, :] = jnp.broadcast_to(base - float((CLASSES - 1) * slots), (8, slots))
     tally[8:, :] = jnp.broadcast_to(0.5 * rel[3:4], (8, width))
 
+    for n in (4, 7, 8, 9):
+        loads[n].wait()
+    order = lax.broadcasted_iota(jnp.int32, (room, slots), 0).astype(f32)
+    picks, high, low = [], [], []
+    for b in range(blocks):
+        picks.append(jnp.where(order == goals[b], 1.0, 0.0).astype(bf16))
+        high.append((spot[b : b + 1] * slots).astype(f32))
+        low.append((at[b : b + 1] + 1).astype(f32))
+    picks = jnp.concatenate(picks, axis=1)
+    high = jnp.broadcast_to(jnp.concatenate(high, axis=1), (slots, senders)).astype(bf16)
+    low = jnp.broadcast_to(jnp.concatenate(low, axis=1), (slots, senders)).astype(bf16)
+    sorted_ids = dot_nt(picks, high) + dot_nt(picks, low)
+    masked[...] = jnp.where(sorted_ids > 0.5, 0.5 * b_edge[...], -1e30).astype(bf16)
+    sorted_ids = sorted_ids.astype(jnp.int32) - 1
+    lanes = lax.broadcasted_iota(jnp.int32, (room, slots), 1)
+
+    cell_x, cell_z = split(lax.broadcasted_iota(jnp.int32, (slots, slots), 0), spans[2])
+    cell_x, cell_y = split(cell_x, spans[1])
+    step = jnp.zeros((slots, width), f32)
+    for c, v in enumerate((cell_x, cell_y, cell_z)):
+        gap = v - 1 if wide(AXES[c]) else v - here[c]
+        step = step + gap.astype(f32) * rel[c : c + 1]
+    step_high = step.astype(bf16)
+    step_low = (step - step_high.astype(f32)).astype(bf16)
+    of_cell = jnp.where(lax.shift_right_arithmetic(sorted_ids, slots.bit_length() - 1) == lanes, 1.0, 0.0).astype(bf16)
+    moved = dot(of_cell, step_high) + dot(of_cell, step_low)
+
     peers = jnp.int32(1 if has_mate else 0)
     for far, _, when in routes:
         cores = 2 if has_mate and far < RELAYED else 1
@@ -244,33 +271,6 @@
     for when, which in [(s[1], s[4]) for s in sends] + [(r[1], r[5]) for r in relays]:
         if when is not None:
             pl.when(jnp.logical_not(when))(functools.partial(clear, which))
-
-    for n in (4, 7, 8, 9):
-        loads[n].wait()
-    order = lax.broadcasted_iota(jnp.int32, (room, slots), 0).astype(f32)
-    picks, high, low = [], [], []
-    for b in range(blocks):
-        picks.append(jnp.where(order == goals[b], 1.0, 0.0).astype(bf16))
-        high.append((spot[b : b + 1] * slots).astype(f32))
-        low.append((at[b : b + 1] + 1).astype(f32))
-    picks = jnp.concatenate(picks, axis=1)
-    high = jnp.broadcast_to(jnp.concatenate(high, axis=1), (slots, senders)).astype(bf16)
-    low = jnp.broadcast_to(jnp.concatenate(low, axis=1), (slots, senders)).astype(bf16)
-    sorted_ids = dot_nt(picks, high) + dot_nt(picks, low)
-    masked[...] = jnp.where(sorted_ids > 0.5, 0.5 * b_edge[...], -1e30).astype(bf16)
-    sorted_ids = sorted_ids.astype(jnp.int32) - 1
-    lanes = lax.broadcasted_iota(jnp.int32, (room, slots), 1)
-
-    cell_x, cell_z = split(lax.broadcasted_iota(jnp.int32, (slots, slots), 0), spans[2])
-    cell_x, cell_y = split(cell_x, spans[1])
-    step = jnp.zeros((slots, width), f32)
-    for c, v in enumerate((cell_x, cell_y, cell_z)):
-        gap = v - 1 if wide(AXES[c]) else v - here[c]
-        step = step + gap.astype(f32) * rel[c : c + 1]
-    step_high = step.astype(bf16)
-    step_low = (step - step_high.astype(f32)).astype(bf16)
-    of_cell = jnp.where(lax.shift_right_arithmetic(sorted_ids, slots.bit_length() - 1) == lanes, 1.0, 0.0).astype(bf16)
-    moved = dot(of_cell, step_high) + dot(of_cell, step_low)
 
     for r, (line, far) in enumerate(lines):
         for k in range(span_z):

time: 16.9 us -> 16.6 us (0.982)
  Pallas kernels: 16.1 us -> 15.7 us
    pallas_call x1, Pallas kernels: 12.2 us -> 11.8 us  [shards(): pl.pallas_call(exchange, out_shape=[jax.ShapeDtypeStruct(*s) for s in bet...]
where the time goes in v3:
time: 16.6 us; the launch traced here: 16.4 us
  Pallas kernels  15.7 us (95%)
  between operations  0.66 us (4%)
    pallas_call x1, Pallas kernels, shards(): pl.pallas_call(exchange, out_shape=[jax.ShapeDtypeStruct(*s) for s in bet...  11.8 us
    pallas_call x1, Pallas kernels, shards(): pl.pallas_call(finish, out_shape=jax.ShapeDtypeStruct(latents.shape, late...  3.91 us

profile of v3, /device:TPU:0, one launch (start us, length us, event | category | flops | bytes accessed | tf_op | source)
XLA Modules:
  0.0 16.4 jit_solution(12759445565566030436)
XLA Ops:
  0.7 11.8 %shard_map.136 = (bf16[640,128]{1,0:T(8,128)(2,1)S(1)}, f32[5,128,128]{2,1,0:T(8,128)S(1)}, f32[128,128]{1,0:T(8,128)S(1)}, bf16[640,128]{1,0:T(8,128)(2,1)S(1)}...) custom-call(s32[1,1,1]{2,1,0:T(1,128)S(6)} %copy.15.refs_0_, ...), custom_call_target="tpu_custom_call" | custom-call | tf_op jit(solution)/shard_map/pallas_call | solution.py:421
  12.5 3.9 %shard_map.137 = bf16[1,1,1,128,128]{4,3,2,1,0:T(8,128)(2,1)} custom-call(bf16[640,128]{1,0:T(8,128)(2,1)S(1)} %get-tuple-element.12.refs_0_, f32[5,128,128]{2,1,0:T(8,128)S(1)} %get-tuple-element.13.refs_1_, f32[128,128]{1,0:T(8,128)S(1)} %get-tuple-element.14.refs_2_, bf16[640,128]{1,0:T(8,128)(2,1)S(1)} %get-tuple-element.15.refs_3_, ...), custom_call_target="tpu_custom_call" | custom-call | tf_op jit(solution)/shard_map/pallas_call | solution.py:441

commit v4 on v3

--- a/solution.py
+++ b/solution.py
@@ -10,7 +10,7 @@
 MESH = pl.DeviceIdType.MESH
 AXES = ("gx", "gy", "gz")
 PACK = 16
-GROUP = 64
+GROUPS = (128, 64, 128)
 CLASSES = 3
 RELAYED = 2
 NT = (((1,), (1,)), ((), ()))
@@ -287,16 +287,17 @@
     place_cols = [jnp.transpose(jnp.broadcast_to(place[c : c + 1], (slots, slots))) for c in range(3)]
 
     def gather(roles, top, bottom):
-        total = moved[top:bottom], jnp.zeros((PACK, bottom - top), f32)
+        total = jnp.concatenate([moved[top:bottom], jnp.zeros((bottom - top, PACK), f32)], axis=1)
         for r in roles:
             picked, cells = chosen[r, top:bottom, :], table.at[pl.ds(lines[r][0] * span_z, span_z)]
-            rows_of = cells[:, :slots, :].reshape(span_z * slots, width)
-            extras = cells[:, slots:, :]
-            extras = jnp.concatenate([extras[k] for k in range(span_z)], axis=1)
-            total = total[0] + dot(picked, rows_of), total[1] + dot_nt(extras, picked)
-        send_half[top:bottom, :] = (0.5 * total[0]).astype(bf16)
+            sides = [jnp.transpose(cells[k, slots:, :].astype(f32)).astype(bf16) for k in range(span_z)]
+            both_of = jnp.concatenate(
+                [cells[:, :slots, :].reshape(span_z * slots, width), jnp.concatenate(sides, axis=0)], axis=1
+            )
+            total = total + dot(picked, both_of)
+        send_half[top:bottom, :] = (0.5 * total[:, :width]).astype(bf16)
         for n in range(top // slots, bottom // slots):
-            feats = total[1][:, n * slots - top : (n + 1) * slots - top]
+            feats = jnp.transpose(total[n * slots - top : (n + 1) * slots - top, width:])
             square = jnp.zeros((slots, slots), f32)
             for c in range(3):
                 where = feats[c : c + 1] + (feats[3 + c : 4 + c] - here[c].astype(f32))
@@ -316,12 +317,14 @@
     def work(block):
         top = block * slots
 
-        @pl.loop(0, slots // GROUP)
+        size = GROUPS[block]
+
+        @pl.loop(0, slots // size)
         def _(group):
-            base = pl.multiple_of(group * GROUP, GROUP)
-            own_rows = recv_half[pl.ds(base, GROUP), :].astype(bf16)
-            near_rows = near[block, pl.ds(base, GROUP), :].astype(bf16)
-            for i in range(0, GROUP, 2):
+            base = pl.multiple_of(group * size, size)
+            own_rows = recv_half[pl.ds(base, size), :].astype(bf16)
+            near_rows = near[block, pl.ds(base, size), :].astype(bf16)
+            for i in range(0, size, 2):
                 edges = edges_of(own_rows[i : i + 2], near_rows[i : i + 2], send_half[top : top + slots, :], rel_half)
                 sums = messages_of(dot(edges, pair_edge[...]), masked[top : top + slots, :])
                 for n in range(2):
@@ -367,19 +370,19 @@
         load.start()
     slots, width = recv_half.shape
     used = jnp.max(tally[:8, :]).astype(jnp.int32)
-    steps = lax.div(used + (slots - 1), jnp.int32(slots)) * (slots // GROUP)
+    steps = lax.div(used + (slots - 1), jnp.int32(slots)) * (slots // GROUPS[-1])
     part[...] = jnp.zeros_like(part)
     rel_half = tally[8:9, :].astype(bf16)
 
     @pl.loop(0, steps)
     def _(step):
-        block, group = split(step, slots // GROUP)
+        block, group = split(step, slots // GROUPS[-1])
         block = block + (CLASSES - 1)
         top = pl.multiple_of(block * slots, slots)
-        base = pl.multiple_of(group * GROUP, GROUP)
-        own_rows = recv_half[pl.ds(base, GROUP), :].astype(bf16)
-        near_rows = near[block, pl.ds(base, GROUP), :].astype(bf16)
-        for i in range(0, GROUP, 2):
+        base = pl.multiple_of(group * GROUPS[-1], GROUPS[-1])
+        own_rows = recv_half[pl.ds(base, GROUPS[-1]), :].astype(bf16)
+        near_rows = near[block, pl.ds(base, GROUPS[-1]), :].astype(bf16)
+        for i in range(0, GROUPS[-1], 2):
             edges = edges_of(own_rows[i : i + 2], near_rows[i : i + 2], send_half[pl.ds(top, slots), :], rel_half)
             sums = messages_of(dot(edges, pair_edge[...]), masked[pl.ds(top, slots), :])
             for n in range(2):

time: 16.6 us -> 16.5 us (level)
  no operation moved by 1% of the time
where the time goes in v4:
time: 16.5 us; the launch traced here: 16.2 us
  Pallas kernels  15.6 us (95%)
  between operations  0.66 us (4%)
    pallas_call x1, Pallas kernels, shards(): pl.pallas_call(exchange, out_shape=[jax.ShapeDtypeStruct(*s) for s in bet...  11.8 us
    pallas_call x1, Pallas kernels, shards(): pl.pallas_call(finish, out_shape=jax.ShapeDtypeStruct(latents.shape, late...  3.81 us

profile of v4, /device:TPU:0, one launch (start us, length us, event | category | flops | bytes accessed | tf_op | source)
XLA Modules:
  0.0 16.2 jit_solution(5023912623443533096)
XLA Ops:
  0.7 11.8 %shard_map.136 = (bf16[640,128]{1,0:T(8,128)(2,1)S(1)}, f32[5,128,128]{2,1,0:T(8,128)S(1)}, f32[128,128]{1,0:T(8,128)S(1)}, bf16[640,128]{1,0:T(8,128)(2,1)S(1)}...) custom-call(s32[1,1,1]{2,1,0:T(1,128)S(6)} %copy.15.refs_0_, ...), custom_call_target="tpu_custom_call" | custom-call | tf_op jit(solution)/shard_map/pallas_call | solution.py:424
  12.4 3.8 %shard_map.137 = bf16[1,1,1,128,128]{4,3,2,1,0:T(8,128)(2,1)} custom-call(bf16[640,128]{1,0:T(8,128)(2,1)S(1)} %get-tuple-element.12.refs_0_, f32[5,128,128]{2,1,0:T(8,128)S(1)} %get-tuple-element.13.refs_1_, f32[128,128]{1,0:T(8,128)S(1)} %get-tuple-element.14.refs_2_, bf16[640,128]{1,0:T(8,128)(2,1)S(1)} %get-tuple-element.15.refs_3_, ...), custom_call_target="tpu_custom_call" | custom-call | tf_op jit(solution)/shard_map/pallas_call | solution.py:444

commit v5 on v4

--- a/solution.py
+++ b/solution.py
@@ -286,8 +286,10 @@
     recv_half[...] = 0.5 * (dot(latent, w_recv[0]) + b_first[...] - shift)
     place_cols = [jnp.transpose(jnp.broadcast_to(place[c : c + 1], (slots, slots))) for c in range(3)]
 
-    def gather(roles, top, bottom):
-        total = jnp.concatenate([moved[top:bottom], jnp.zeros((bottom - top, PACK), f32)], axis=1)
+    def begin(top, bottom):
+        return jnp.concatenate([moved[top:bottom], jnp.zeros((bottom - top, PACK), f32)], axis=1)
+
+    def pick(roles, top, bottom, total):
         for r in roles:
             picked, cells = chosen[r, top:bottom, :], table.at[pl.ds(lines[r][0] * span_z, span_z)]
             sides = [jnp.transpose(cells[k, slots:, :].astype(f32)).astype(bf16) for k in range(span_z)]
@@ -295,6 +297,9 @@
                 [cells[:, :slots, :].reshape(span_z * slots, width), jnp.concatenate(sides, axis=0)], axis=1
             )
             total = total + dot(picked, both_of)
+        return total
+
+    def store(total, top, bottom):
         send_half[top:bottom, :] = (0.5 * total[:, :width]).astype(bf16)
         for n in range(top // slots, bottom // slots):
             feats = jnp.transpose(total[n * slots - top : (n + 1) * slots - top, width:])
@@ -335,6 +340,8 @@
                 pl.when(group == 0)(pass_on)
 
     for far in range(CLASSES):
+        top, bottom = far * slots, room if far == CLASSES - 1 else (far + 1) * slots
+        total = pick([r for r, (_, step_far) in enumerate(lines) if step_far < far], top, bottom, begin(top, bottom))
         if has_mate and far == 0:
             mate_in.wait_recv()
         for step_far, when, _, arrival, _ in sends:
@@ -343,8 +350,8 @@
         for step_far, when, _, _, twin_in, _ in relays:
             if step_far == far:
                 guarded(when, twin_in.wait_recv)
-        roles = [r for r, (_, step_far) in enumerate(lines) if step_far <= far]
-        gather(roles, far * slots, room if far == CLASSES - 1 else (far + 1) * slots)
+        total = pick([r for r, (_, step_far) in enumerate(lines) if step_far == far], top, bottom, total)
+        store(total, top, bottom)
         if far < CLASSES - 1:
             work(far)
         if far == CLASSES - 2:

time: 16.5 us -> 16.6 us (level)
  no operation moved by 1% of the time
where the time goes in v5:
time: 16.6 us; the launch traced here: 16.4 us
  Pallas kernels  15.7 us (95%)
  between operations  0.66 us (4%)
    pallas_call x1, Pallas kernels, shards(): pl.pallas_call(exchange, out_shape=[jax.ShapeDtypeStruct(*s) for s in bet...  11.9 us
    pallas_call x1, Pallas kernels, shards(): pl.pallas_call(finish, out_shape=jax.ShapeDtypeStruct(latents.shape, late...  3.81 us

profile of v5, /device:TPU:0, one launch (start us, length us, event | category | flops | bytes accessed | tf_op | source)
XLA Modules:
  0.0 16.4 jit_solution(3785782568552681129)
XLA Ops:
  0.7 11.9 %shard_map.136 = (bf16[640,128]{1,0:T(8,128)(2,1)S(1)}, f32[5,128,128]{2,1,0:T(8,128)S(1)}, f32[128,128]{1,0:T(8,128)S(1)}, bf16[640,128]{1,0:T(8,128)(2,1)S(1)}...) custom-call(s32[1,1,1]{2,1,0:T(1,128)S(6)} %copy.15.refs_0_, ...), custom_call_target="tpu_custom_call" | custom-call | tf_op jit(solution)/shard_map/pallas_call | solution.py:431
  12.6 3.8 %shard_map.137 = bf16[1,1,1,128,128]{4,3,2,1,0:T(8,128)(2,1)} custom-call(bf16[640,128]{1,0:T(8,128)(2,1)S(1)} %get-tuple-element.12.refs_0_, f32[5,128,128]{2,1,0:T(8,128)S(1)} %get-tuple-element.13.refs_1_, f32[128,128]{1,0:T(8,128)S(1)} %get-tuple-element.14.refs_2_, bf16[640,128]{1,0:T(8,128)(2,1)S(1)} %get-tuple-element.15.refs_3_, ...), custom_call_target="tpu_custom_call" | custom-call | tf_op jit(solution)/shard_map/pallas_call | solution.py:451
